TPU v7x, 512 devices: a whole 4x8x8 slice. The times are simulated.
512 devices in a mesh: dp: 64 (over y, x, core), mp: 8 (over z).
Axes of the slice: x: 4, y: 8, z: 8, core: 2. Of those that a mesh axis runs over, the one named last changes fastest.
Arguments:
- hidden: bfloat16 [960, 128, 2048], P('dp', None, 'mp'), may hold values from -6 to 6
- attn_out: bfloat16 [960, 128, 2048], P('dp', None, 'mp'), may hold values from -6 to 6
- out_proj: bfloat16 [2048, 2048], P(None, 'mp'), may hold values from -0.125 to 0.125
- norm_gain: float32 [2048], P('mp'), may hold values from 0.1 to 1.9
- reward_proj: float32 [2048, 8], P('mp'), may hold values from -0.125 to 0.125
- block_seq: int32 [960], replicated, may hold values from -1 to 383, as said below
- block_dest: int32 [960], replicated, may hold values from -1 to 639, as said below
- lengths: int32 [384], replicated, may hold values from 1 to 512, as said below
Outputs:
- token_rewards: float32 [640, 8, 128], P('dp')
- advantages: float32 [384], P('dp')
Inputs may be any that keep to these rules, and one draw needn't show every extreme that they name: `block_seq`: used slots of each index of dp come first in its 15 slots, the rest hold -1; each index of dp holds 1 to 15 used slots and some index holds exactly 15. Read over used slots in slot order, response numbers never fall, every response appears, and each has 1 to 4 blocks. `block_dest`: exactly the used slots (those of block_seq that are not -1) hold a destination; every owned slot of every owner is named exactly once, so each owner receives exactly 10 blocks; at most 1 block go from one index of dp to one owner, and that many in some pair. `lengths`: A response of n blocks has more than 128 * (n - 1) and at most 128 * n tokens.
All inputs are finite; a program needn't handle non-finite values.
Results may differ from a plain program's by a relative error of at most 0.0029.
Values may be sent and summed in bfloat16 or wider, within the bound.
No kernel may reach another device: no remote copies, remote signals or barrier semaphores. Data moves between devices by JAX's collectives and lax.ppermute only.
A program may use at most 64 MiB of HBM per device.

v0:
```python
import jax
import jax.numpy as jnp
from jax import lax
from jax.sharding import PartitionSpec as P

OWN_CAP = 10
norm_epsilon = 1e-05
stat_epsilon = 1e-06


def sent_to_all(value, axis):
    copies = jnp.broadcast_to(value, (lax.axis_size(axis), *value.shape))
    return lax.all_to_all(copies, axis, split_axis=0, concat_axis=0, tiled=True)


def of_everyone(value, axis):
    everything = sent_to_all(value, axis)
    return jnp.sum(everything, axis=0)


def packed_total(arrays, axis):
    ends = [0]
    for a in arrays:
        ends.append(ends[-1] + a.size)
    so_far = of_everyone(jnp.concatenate([a.ravel() for a in arrays]), axis)
    return tuple((so_far[b:e].reshape(a.shape) for a, b, e in zip(arrays, ends, ends[1:])))


def split_up(value, dim, peers):
    before, after = (value.shape[:dim], value.shape[dim + 1 :])
    return jnp.moveaxis(value.reshape(*before, peers, -1, *after), dim, 0)


def sent_and_summed(value, axis, dim):
    parts = split_up(value, dim, lax.axis_size(axis))
    arrived = lax.all_to_all(parts, axis, split_axis=0, concat_axis=0, tiled=True)
    return arrived.sum(axis=0)


def local(hidden, attn_out, out_proj, norm_gain, reward_proj, block_seq, block_dest, lengths):
    device_count = lax.axis_size("dp")
    device_rank = lax.axis_index("dp")
    slots_in = hidden.shape[0]
    block_len = hidden.shape[1]
    model_width = out_proj.shape[0]
    seq_count = lengths.shape[0]
    seq_local = seq_count // device_count
    slot_depth = (slots_in + device_count - 1) // device_count
    all_slots = jnp.arange(block_dest.shape[0], dtype=jnp.int32)
    local_dest = lax.dynamic_slice_in_dim(block_dest, device_rank * slots_in, slots_in)
    is_used = local_dest >= 0
    owner_rank = jnp.where(is_used, local_dest // OWN_CAP, -1)
    local_slots = jnp.arange(slots_in, dtype=jnp.int32)
    earlier = (
        (owner_rank[None, :] == owner_rank[:, None])
        & (local_slots[None, :] < local_slots[:, None])
        & is_used[None, :]
    )
    send_row = jnp.where(is_used, owner_rank * slot_depth + earlier.sum(axis=1), -1)
    buffer_rows = jnp.arange(device_count * slot_depth, dtype=jnp.int32)
    selector = (send_row[None, :] == buffer_rows[:, None]).astype(jnp.bfloat16)
    targets = device_rank * OWN_CAP + jnp.arange(OWN_CAP, dtype=jnp.int32)
    matches = block_dest[None, :] == targets[:, None]
    source_slot = jnp.sum(jnp.where(matches, all_slots[None, :], 0), axis=1)
    source_rank = source_slot // slots_in
    before = (block_dest[None, :] >= 0) & (block_dest[None, :] // OWN_CAP == device_rank)
    before = (
        before
        & (all_slots[None, :] >= (source_rank * slots_in)[:, None])
        & (all_slots[None, :] < source_slot[:, None])
    )
    recv_row = source_rank * slot_depth + before.sum(axis=1)
    seq_own = jnp.sum(jnp.where(matches, block_seq[None, :], 0), axis=1)
    earlier_same = (block_seq[None, :] == seq_own[:, None]) & (
        all_slots[None, :] < source_slot[:, None]
    )
    seq_rank = earlier_same.sum(axis=1)
    seq_ids = jnp.arange(seq_count, dtype=jnp.int32)
    member = seq_ids[:, None] == seq_own[None, :]
    own_length = jnp.sum(jnp.where(member, lengths[:, None], 0), axis=0)
    valid_tokens = jnp.minimum(block_len, own_length - block_len * seq_rank)
    projected = jnp.einsum(
        "btf,fc->btc",
        lax.all_gather(attn_out, "mp", axis=2, tiled=True),
        out_proj,
        preferred_element_type=jnp.float32,
    )
    local_resid = (hidden.astype(jnp.float32) + projected).astype(jnp.bfloat16)
    moved_resid = lax.all_to_all(
        jnp.einsum("rj,jtf->rtf", selector, local_resid, preferred_element_type=jnp.float32).astype(
            jnp.bfloat16
        ),
        "dp",
        split_axis=0,
        concat_axis=0,
        tiled=True,
    )
    residual = jnp.take(moved_resid, recv_row, axis=0)
    values = residual.astype(jnp.float32)
    squares = jnp.sum(values * values, axis=2)
    weighted = norm_gain[:, None] * reward_proj
    partial_value = jnp.einsum("btf,fh->bht", values, weighted, precision=lax.Precision.HIGHEST)
    squares, partial_value = packed_total((squares, partial_value), "mp")
    inverse_rms = lax.rsqrt(squares / model_width + norm_epsilon)
    live_tokens = (jnp.arange(block_len, dtype=jnp.int32)[None, :] < valid_tokens[:, None]).astype(
        jnp.float32
    )
    token_rewards = partial_value * (inverse_rms * live_tokens)[:, None, :]
    block_sums = jnp.sum(token_rewards, axis=2)
    seq_part = jnp.dot(member.astype(jnp.float32), block_sums, precision=lax.Precision.HIGHEST)
    seq_totals = sent_and_summed(seq_part, "dp", 0)
    own_lengths = lax.dynamic_slice_in_dim(lengths, device_rank * seq_local, seq_local).astype(
        jnp.float32
    )
    scores = seq_totals / own_lengths[:, None]
    worst_case = jnp.min(scores, axis=1)
    head_mean = jnp.mean(scores, axis=1)
    spread = jnp.mean((scores - head_mean[:, None]) ** 2, axis=1)
    total_seqs = float(seq_count)
    moment_sums = packed_total(
        (
            jnp.sum(spread),
            jnp.sum(worst_case),
            jnp.sum(worst_case * worst_case),
            jnp.sum(worst_case * spread),
            jnp.sum(spread * spread),
        ),
        "dp",
    )
    penalty_scale = moment_sums[0] / total_seqs + stat_epsilon
    conservative = worst_case - spread / penalty_scale
    first_sum = moment_sums[1] - moment_sums[0] / penalty_scale
    second = (
        moment_sums[2]
        - 2.0 * moment_sums[3] / penalty_scale
        + moment_sums[4] / (penalty_scale * penalty_scale)
    )
    centre = first_sum / total_seqs
    variance = second / total_seqs - centre * centre
    advantages = (conservative - centre) * lax.rsqrt(variance + stat_epsilon)
    return (token_rewards, advantages)


def solution(mesh):
    return jax.shard_map(
        local,
        mesh=mesh,
        in_specs=(
            P("dp", None, "mp"),
            P("dp", None, "mp"),
            P(None, "mp"),
            P("mp"),
            P("mp", None),
            P(),
            P(),
            P(),
        ),
        out_specs=(P("dp", None, None), P("dp")),
        check_vma=False,
    )
```

profile of v0, /device:TPU:1, one launch (start us, length us, event | category | flops | bytes accessed | tf_op | source)
XLA Modules:
  0.0 305.1 jit_solution(17338030331236136521)
XLA Ops:
  7.2 0.0 copy-start
  7.2 0.0 all-gather.2.cloned.1.call-start
  7.2 0.7 all-gather.2.cloned.1.call-update
  7.9 0.8 fusion.29
  8.7 0.2 convert_reduce_fusion.2
  8.9 101.2 %all-gather.2.cloned.1.call-done = bf16[15,128,2048]{2,1,0:T(8,128)(2,1)} async-done(((bf16[15,128,256]{2,1,0:T(8,128)(2,1)}), bf16[15,128,2048]{2,1,0:T(8,128)(2,1)}) %all-gather.2.cloned.1.call-update) | async-done | bytes 7864336 | tf_op jit(solution)/shard_map/all_gather | solution.py:84
  110.1 0.0 copy-done
  110.1 5.7 %add_convert_fusion = bf16[15,128,256]{2,1,0:T(8,128)(2,1)S(1)} fusion(bf16[15,128,256]{2,1,0:T(8,128)(2,1)} %param.8, bf16[15,128,2048]{2,1,0:T(8,128)(2,1)} %all-gather.2.cloned.1.call-done, bf16[2048,256]{1,0:T(8,128)(2,1)S(1)} %copy-done), kind=kOutput, calls=%fused_computation.3 | convolution fusion | flops 2014740480 | bytes 10878976 | tf_op jit(solution)/shard_map/btf,fc->btc/dot_general | solution.py:82
  115.8 1.4 convolution_convert_fusion
  117.1 4.4 %copy.29 = bf16[64,128,256]{2,1,0:T(8,128)(2,1)} copy(bf16[64,128,256]{2,0,1:T(8,128)(2,1)S(1)} %convolution_convert_fusion) | data formatting | bytes 8388608 | tf_op jit(solution)/shard_map/convert_element_type | solution.py:90
  121.5 0.0 copy-start.1
  121.5 0.0 copy-start.2
  121.5 0.0 copy-start.4
  121.5 0.0 copy-start.5
  121.5 13.3 %all-to-all-start = ((bf16[64,128,256]{2,1,0:T(8,128)(2,1)}), bf16[64,128,256]{2,1,0:T(8,128)(2,1)}, u32[]{:S(2)}, u32[]{:S(2)}) async-start(bf16[64,128,256]{2,1,0:T(8,128)(2,1)} %copy.29), calls=%async_computation | async-start | bytes 8388608 | tf_op jit(solution)/shard_map/all_to_all | solution.py:89
  134.8 0.0 copy-start.3
  134.9 0.0 copy-done.1
  134.9 0.0 copy-done.2
  134.9 0.2 fusion.3
  135.1 0.2 convert_reduce_fusion
  135.4 94.2 %all-to-all-done = bf16[64,128,256]{2,1,0:T(8,128)(2,1)} async-done(((bf16[64,128,256]{2,1,0:T(8,128)(2,1)}), bf16[64,128,256]{2,1,0:T(8,128)(2,1)}, u32[]{:S(2)}, u32[]{:S(2)}) %all-to-all-start) | async-done | bytes 4194336 | tf_op jit(solution)/shard_map/all_to_all | solution.py:89
  229.5 2.8 gather_fusion
  232.3 0.3 multiply_reduce_fusion
  232.7 0.0 copy-done.4
  232.7 0.0 copy-done.5
  232.7 0.7 convolution_bitcast_fusion
  233.4 0.9 broadcast_in_dim.89
  234.3 3.9 %all-to-all-start.1 = ((f32[8,1,11520]{2,1,0:T(1,128)}), f32[8,1,11520]{2,1,0:T(1,128)S(1)}, u32[]{:S(2)}, u32[]{:S(2)}) async-start(f32[8,1,11520]{2,1,0:T(1,128)} %broadcast_in_dim.89), calls=%async_computation.1 | async-start | bytes 737280 | tf_op jit(solution)/shard_map/all_to_all | solution.py:13
  238.2 0.0 copy-done.3
  238.2 0.2 select_reduce_fusion
  238.4 11.5 %all-to-all-done.1 = f32[8,1,11520]{2,1,0:T(1,128)S(1)} async-done(((f32[8,1,11520]{2,1,0:T(1,128)}), f32[8,1,11520]{2,1,0:T(1,128)S(1)}, u32[]{:S(2)}, u32[]{:S(2)}) %all-to-all-start.1) | async-done | bytes 368672 | tf_op jit(solution)/shard_map/all_to_all | solution.py:13
  249.9 0.3 reduce_sum.169
  250.2 0.1 fusion.15
  250.2 0.6 fusion.34
  250.9 0.2 fusion.7
  251.1 0.8 copy.32
  251.9 9.6 %all-to-all-start.2 = ((f32[64,6,8]{2,1,0:T(8,128)}), f32[64,6,8]{2,1,0:T(8,128)S(1)}, u32[]{:S(2)}, u32[]{:S(2)}) async-start(f32[64,6,8]{2,1,0:T(8,128)} %copy.32), calls=%async_computation.2 | async-start | bytes 524288 | tf_op jit(solution)/shard_map/all_to_all | solution.py:36
  261.6 0.1 dynamic-slice_convert_fusion
  261.6 13.0 %all-to-all-done.2 = f32[64,6,8]{2,1,0:T(8,128)S(1)} async-done(((f32[64,6,8]{2,1,0:T(8,128)}), f32[64,6,8]{2,1,0:T(8,128)S(1)}, u32[]{:S(2)}, u32[]{:S(2)}) %all-to-all-start.2) | async-done | bytes 12320 | tf_op jit(solution)/shard_map/all_to_all | solution.py:36
  274.6 0.1 reduce_sum.174
  274.7 0.2 fusion.32
  274.9 0.2 multiply_reduce_fusion.1
  275.1 0.7 multiply_reduce_fusion.2
  275.8 3.2 %concatenate.7 = f32[5]{0:T(128)S(1)} concatenate(f32[1]{0:T(128)} %bitcast.13, f32[1]{0:T(128)} %bitcast.14, f32[1]{0:T(128)} %bitcast.15, f32[1]{0:T(128)} %bitcast.16, f32[1]{0:T(128)} %bitcast.17), dimensions={0} | concatenate | bytes 40 | tf_op jit(solution)/shard_map/concatenate | solution.py:25
  279.1 14.0 %all_to_all.22 = f32[64,1,5]{2,1,0:T(1,128)S(1)} all-to-all(f32[64,1,5]{2,1,0:T(1,128)S(1)} %broadcast_in_dim.93), channel_id=1, replica_groups=mesh['dp'=64,'mp'=8] {'dp'}, dimensions={0} | all-to-all | bytes 2560 | tf_op jit(solution)/shard_map/all_to_all | solution.py:13
  293.1 0.1 reduce_sum.182
  293.1 0.7 fusion.36
  297.7 0.5 subtract_multiply_fusion
  (12 shorter events, 0.1 us)
Async XLA Ops:
  7.2 102.9 %copy-start = (bf16[2048,256]{1,0:T(8,128)(2,1)S(1)}, bf16[2048,256]{1,0:T(8,128)(2,1)}, u32[]{:S(2)}) copy-start(bf16[2048,256]{1,0:T(8,128)(2,1)} %param.10) | copy-start | bytes 3145732
  7.2 102.9 %all-gather.2.cloned.1.call-start = ((), (), s32[]{:S(2)}) async-start(), calls=%async_computation.4 | async-start | bytes 8847360 | tf_op jit(solution)/shard_map/all_gather | solution.py:84
  121.5 13.3 %copy-start.1 = (s32[960]{0:T(1024)S(1)}, s32[960]{0:T(1024)}, u32[]{:S(2)}) copy-start(s32[960]{0:T(1024)} %param.14) | copy-start | bytes 11524
  121.5 13.3 %copy-start.2 = (s32[960]{0:T(1024)S(1)}, s32[960]{0:T(1024)}, u32[]{:S(2)}) copy-start(s32[960]{0:T(1024)} %param.13) | copy-start | bytes 11524
  121.5 111.1 %copy-start.4 = (f32[256,8]{0,1:T(8,128)S(1)}, f32[256,8]{0,1:T(8,128)}, u32[]{:S(2)}) copy-start(f32[256,8]{0,1:T(8,128)} %param.12) | copy-start | bytes 24580
  121.5 111.1 %copy-start.5 = (f32[256]{0:T(256)S(1)}, f32[256]{0:T(256)}, u32[]{:S(2)}) copy-start(f32[256]{0:T(256)} %param.11) | copy-start | bytes 3076
  121.5 108.0 %all-to-all-start = ((bf16[64,128,256]{2,1,0:T(8,128)(2,1)}), bf16[64,128,256]{2,1,0:T(8,128)(2,1)}, u32[]{:S(2)}, u32[]{:S(2)}) async-start(bf16[64,128,256]{2,1,0:T(8,128)(2,1)} %copy.29), calls=%async_computation | async-start | bytes 8388608 | tf_op jit(solution)/shard_map/all_to_all | solution.py:89
  134.8 103.4 %copy-start.3 = (s32[384]{0:T(512)S(1)}, s32[384]{0:T(512)}, u32[]{:S(2)}) copy-start(s32[384]{0:T(512)} %param.15) | copy-start | bytes 4612
  234.3 15.6 %all-to-all-start.1 = ((f32[8,1,11520]{2,1,0:T(1,128)}), f32[8,1,11520]{2,1,0:T(1,128)S(1)}, u32[]{:S(2)}, u32[]{:S(2)}) async-start(f32[8,1,11520]{2,1,0:T(1,128)} %broadcast_in_dim.89), calls=%async_computation.1 | async-start | bytes 737280 | tf_op jit(solution)/shard_map/all_to_all | solution.py:13
  251.9 22.7 %all-to-all-start.2 = ((f32[64,6,8]{2,1,0:T(8,128)}), f32[64,6,8]{2,1,0:T(8,128)S(1)}, u32[]{:S(2)}, u32[]{:S(2)}) async-start(f32[64,6,8]{2,1,0:T(8,128)} %copy.32), calls=%async_computation.2 | async-start | bytes 524288 | tf_op jit(solution)/shard_map/all_to_all | solution.py:36
Sparse Core Ops, SparseCore 0:
  10.0 100.0 all-gather.1
where the time goes:
time: 306 us; the launch traced here: 305 us
  waiting for transfers between devices  221 us (72%)
  starting transfers between devices  26.8 us (9%)
  between operations  18.1 us (6%)
  blocking collectives  14 us (5%)
  local copies, waits for them, and re-layouts  12.9 us (4%)
  matrix products  7.93 us (3%)
  other arithmetic  4.83 us (2%)
    all_gather x1, waiting for transfers between devices, local(): lax.all_gather(attn_out, 'mp', axis=2, tiled=True)  101 us
    all_to_all x1, waiting for transfers between devices, local(): lax.all_to_all(jnp.einsum('rj,jtf->rtf', selector, local_resid, preferred...  94.2 us
    all_to_all x1, blocking collectives, sent_to_all(): return lax.all_to_all(copies, axis, split_axis=0, concat_axis=0, tiled=True)  14 us
    all_to_all x1, starting transfers between devices, local(): lax.all_to_all(jnp.einsum('rj,jtf->rtf', selector, local_resid, preferred...  13.3 us
    all_to_all x1, waiting for transfers between devices, sent_and_summed(): lax.all_to_all(parts, axis, split_axis=0, concat_axis=0, tiled=True)  13 us
    all_to_all x1, waiting for transfers between devices, sent_to_all(): return lax.all_to_all(copies, axis, split_axis=0, concat_axis=0, tiled=True)  11.5 us
    all_to_all x1, starting transfers between devices, sent_and_summed(): lax.all_to_all(parts, axis, split_axis=0, concat_axis=0, tiled=True)  9.64 us
  transfers between devices with their start and end apart: 4, of which 4 were waited for; matrix products, arithmetic and copies ran while one was open for 1% of the time, Pallas kernels for 0%

commit v1 on v0

--- a/solution.py
+++ b/solution.py
@@ -6,6 +6,22 @@
 OWN_CAP = 10
 norm_epsilon = 1e-05
 stat_epsilon = 1e-06
+
+
+def product_in_turn(array, axis, dim, product):
+    size, index, rows = (lax.axis_size(axis), lax.axis_index(axis), array.shape[dim])
+    forward = [(i, (i + 1) % size) for i in range(size)]
+    left = [(i, (i - 1) % size) for i in range(size)]
+    halfway = size // 2
+    from_left = from_right = array
+    total = product(array, index * rows)
+    for turn in range(1, halfway + 1):
+        from_left = lax.ppermute(from_left, axis, forward)
+        if turn < size - halfway:
+            from_right = lax.ppermute(from_right, axis, left)
+            total = total + product(from_right, (index + turn) % size * rows)
+        total = total + product(from_left, (index - turn) % size * rows)
+    return total
 
 
 def sent_to_all(value, axis):
@@ -79,11 +95,16 @@
     member = seq_ids[:, None] == seq_own[None, :]
     own_length = jnp.sum(jnp.where(member, lengths[:, None], 0), axis=0)
     valid_tokens = jnp.minimum(block_len, own_length - block_len * seq_rank)
-    projected = jnp.einsum(
-        "btf,fc->btc",
-        lax.all_gather(attn_out, "mp", axis=2, tiled=True),
-        out_proj,
-        preferred_element_type=jnp.float32,
+    projected = product_in_turn(
+        attn_out,
+        "mp",
+        2,
+        lambda part, at: jnp.einsum(
+            "btf,fc->btc",
+            part,
+            lax.dynamic_slice_in_dim(out_proj, at, part.shape[2], axis=0),
+            preferred_element_type=jnp.float32,
+        ),
     )
     local_resid = (hidden.astype(jnp.float32) + projected).astype(jnp.bfloat16)
     moved_resid = lax.all_to_all(

time: 306 us -> 294 us (0.961)
  waiting for transfers between devices: 221 us -> 185 us
  starting transfers between devices: 26.8 us -> 55.7 us
  between operations: 18.1 us -> 5.08 us
  matrix products: 7.93 us -> 11.6 us
  local copies, waits for them, and re-layouts: 12.9 us -> 16.3 us
    all_gather x1 -> x0, waiting for transfers between devices: 101 us -> none  [local(): lax.all_gather(attn_out, 'mp', axis=2, tiled=True)]
    ppermute x0 -> x7, waiting for transfers between devices: none -> 66.6 us  [the longest x4 66.6 us: product_in_turn(): from_left = lax.ppermute(from_left, axis, forward)]
    ppermute x0 -> x7, starting transfers between devices: none -> 28.4 us  [the longest x3 17.7 us: product_in_turn(): from_right = lax.ppermute(from_right, axis, left)]
    dot_general x1 -> x8, matrix products: 5.65 us -> 9.31 us  [local(): jnp.einsum('btf,fc->btc', part, lax.dynamic_slice_in_dim(out_proj, at, pa...]
  transfers between devices with their start and end apart: 4 -> 10, of which waited for: 4 -> 7; matrix products, arithmetic and copies ran while one was open for 1% -> 4% of each run, Pallas kernels for 0% -> 0%
where the time goes in v1:
time: 294 us; the launch traced here: 293 us
  waiting for transfers between devices  185 us (63%)
  starting transfers between devices  55.7 us (19%)
  local copies, waits for them, and re-layouts  16.3 us (6%)
  blocking collectives  14 us (5%)
  matrix products  11.6 us (4%)
  between operations  5.08 us (2%)
  other arithmetic  4.83 us (2%)
    all_to_all x1, waiting for transfers between devices, local(): lax.all_to_all(jnp.einsum('rj,jtf->rtf', selector, local_resid, preferred...  94.1 us
    ppermute x4, waiting for transfers between devices, product_in_turn(): from_left = lax.ppermute(from_left, axis, forward)  66.6 us
    ppermute x3, starting transfers between devices, product_in_turn(): from_right = lax.ppermute(from_right, axis, left)  17.7 us
    all_to_all x1, starting transfers between devices, local(): lax.all_to_all(jnp.einsum('rj,jtf->rtf', selector, local_resid, preferred...  14.3 us
    all_to_all x1, blocking collectives, sent_to_all(): return lax.all_to_all(copies, axis, split_axis=0, concat_axis=0, tiled=True)  14 us
    all_to_all x1, waiting for transfers between devices, sent_and_summed(): lax.all_to_all(parts, axis, split_axis=0, concat_axis=0, tiled=True)  13 us
    all_to_all x1, waiting for transfers between devices, sent_to_all(): return lax.all_to_all(copies, axis, split_axis=0, concat_axis=0, tiled=True)  11.4 us
    ppermute x4, starting transfers between devices, product_in_turn(): from_left = lax.ppermute(from_left, axis, forward)  10.7 us
  transfers between devices with their start and end apart: 10, of which 7 were waited for; matrix products, arithmetic and copies ran while one was open for 4% of the time, Pallas kernels for 0%

profile of v1, /device:TPU:1, one launch (start us, length us, event | category | flops | bytes accessed | tf_op | source)
XLA Modules:
  0.0 292.6 jit_solution(2970092903370639773)
XLA Ops:
  0.6 0.0 copy-start
  0.7 4.9 %collective-permute-start.1 = (bf16[15,128,256]{2,1,0:T(8,128)(2,1)}, bf16[15,128,256]{2,1,0:T(8,128)(2,1)S(1)}, u32[]{:S(2)}, u32[]{:S(2)}) collective-permute-start(bf16[15,128,256]{2,1,0:T(8,128)(2,1)} %param.9), channel_id=1, source_target_pairs={{0,1},{1,2},{2,3},{3,4},{4,5},{5,6},{6,7},{7,0},{8,9},{9,10},{10,1... | collective-permute-start | bytes 2949128 | tf_op jit(solution)/shard_map/ppermute | solution.py:19
  5.6 8.6 %collective-permute-start = (bf16[15,128,256]{2,1,0:T(8,128)(2,1)}, bf16[15,128,256]{2,1,0:T(8,128)(2,1)}, u32[]{:S(2)}, u32[]{:S(2)}) collective-permute-start(bf16[15,128,256]{2,1,0:T(8,128)(2,1)} %param.9), channel_id=1, source_target_pairs={{0,7},{1,0},{2,1},{3,2},{4,3},{5,4},{6,5},{7,6},{8,15},{9,8},{10,9... | collective-permute-start | bytes 2949128 | tf_op jit(solution)/shard_map/ppermute | solution.py:21
  14.2 19.7 %collective-permute-done.1 = bf16[15,128,256]{2,1,0:T(8,128)(2,1)S(1)} collective-permute-done((bf16[15,128,256]{2,1,0:T(8,128)(2,1)}, bf16[15,128,256]{2,1,0:T(8,128)(2,1)S(1)}, u32[]{:S(2)}, u32[]{:S(2)}) %collective-permute-start.1) | collective-permute-done | bytes 983072 | tf_op jit(solution)/shard_map/ppermute | solution.py:19
  33.9 1.9 collective-permute-start.3
  35.9 0.0 collective-permute-done
  35.9 4.6 %collective-permute-start.2 = (bf16[15,128,256]{2,1,0:T(8,128)(2,1)}, bf16[15,128,256]{2,1,0:T(8,128)(2,1)}, u32[]{:S(2)}, u32[]{:S(2)}) collective-permute-start(bf16[15,128,256]{2,1,0:T(8,128)(2,1)} %collective-permute-done), channel_id=1, source_target_pairs={{0,7},{1,0},{2,1},{3,2},{4,3},{5,4},{6,5},{7,6},{8,15},{9,8},{10,9... | collective-permute-start | bytes 2949128 | tf_op jit(solution)/shard_map/ppermute | solution.py:21
  40.5 0.8 fusion.59
  41.2 0.2 convert_reduce_fusion.2
  41.4 17.8 %collective-permute-done.3 = bf16[15,128,256]{2,1,0:T(8,128)(2,1)} collective-permute-done((bf16[15,128,256]{2,1,0:T(8,128)(2,1)S(1)}, bf16[15,128,256]{2,1,0:T(8,128)(2,1)}, u32[]{:S(2)}, u32[]{:S(2)}) %collective-permute-start.3) | collective-permute-done | bytes 983072 | tf_op jit(solution)/shard_map/ppermute | solution.py:19
  59.2 1.9 collective-permute-start.5
  61.3 1.6 copy.55
  62.9 0.0 copy-done
  62.9 0.0 copy-done.1
  62.9 0.0 copy-start.3
  62.9 0.5 fusion.14
  63.4 0.7 copy-done.3
  64.1 0.5 fusion.10
  64.6 0.0 collective-permute-done.2
  64.6 4.6 %collective-permute-start.4 = (bf16[15,128,256]{2,1,0:T(8,128)(2,1)}, bf16[15,128,256]{2,1,0:T(8,128)(2,1)S(1)}, u32[]{:S(2)}, u32[]{:S(2)}) collective-permute-start(bf16[15,128,256]{2,1,0:T(8,128)(2,1)} %collective-permute-done.2), channel_id=1, source_target_pairs={{0,7},{1,0},{2,1},{3,2},{4,3},{5,4},{6,5},{7,6},{8,15},{9,8},{10,9... | collective-permute-start | bytes 2949128 | tf_op jit(solution)/shard_map/ppermute | solution.py:21
  69.2 1.7 fusion.12
  70.9 12.9 %collective-permute-done.5 = bf16[15,128,256]{2,1,0:T(8,128)(2,1)} collective-permute-done((bf16[15,128,256]{2,1,0:T(8,128)(2,1)}, bf16[15,128,256]{2,1,0:T(8,128)(2,1)}, u32[]{:S(2)}, u32[]{:S(2)}) %collective-permute-start.5) | collective-permute-done | bytes 983072 | tf_op jit(solution)/shard_map/ppermute | solution.py:19
  83.8 1.9 collective-permute-start.6
  85.7 1.7 fusion.6
  87.4 1.7 fusion.8
  89.1 1.7 fusion.2
  90.8 0.0 collective-permute-done.4
  90.8 0.5 fusion.4
  91.3 16.2 %collective-permute-done.6 = bf16[15,128,256]{2,1,0:T(8,128)(2,1)S(1)} collective-permute-done((bf16[15,128,256]{2,1,0:T(8,128)(2,1)}, bf16[15,128,256]{2,1,0:T(8,128)(2,1)S(1)}, u32[]{:S(2)}, u32[]{:S(2)}) %collective-permute-start.6) | collective-permute-done | bytes 983072 | tf_op jit(solution)/shard_map/ppermute | solution.py:19
  107.5 1.1 fusion
  108.6 1.1 copy.64
  109.7 1.4 convolution_convert_fusion
  111.0 4.4 %copy.65 = bf16[64,128,256]{2,1,0:T(8,128)(2,1)} copy(bf16[64,128,256]{2,0,1:T(8,128)(2,1)S(1)} %convolution_convert_fusion) | data formatting | bytes 8388608 | tf_op jit(solution)/shard_map/convert_element_type | solution.py:111
  115.4 14.3 %all-to-all-start = ((bf16[64,128,256]{2,1,0:T(8,128)(2,1)}), bf16[64,128,256]{2,1,0:T(8,128)(2,1)}, u32[]{:S(2)}, u32[]{:S(2)}) async-start(bf16[64,128,256]{2,1,0:T(8,128)(2,1)} %copy.65), calls=%async_computation | async-start | bytes 8388608 | tf_op jit(solution)/shard_map/all_to_all | solution.py:110
  129.7 0.0 copy-start.7
  129.7 0.0 copy-start.8
  129.8 0.2 fusion.25
  130.0 0.2 convert_reduce_fusion
  130.3 0.0 copy-start.6
  130.3 94.1 %all-to-all-done = bf16[64,128,256]{2,1,0:T(8,128)(2,1)} async-done(((bf16[64,128,256]{2,1,0:T(8,128)(2,1)}), bf16[64,128,256]{2,1,0:T(8,128)(2,1)}, u32[]{:S(2)}, u32[]{:S(2)}) %all-to-all-start) | async-done | bytes 4194336 | tf_op jit(solution)/shard_map/all_to_all | solution.py:110
  224.4 2.8 gather_fusion
  227.2 0.3 multiply_reduce_fusion
  227.5 0.7 convolution_bitcast_fusion
  228.3 0.9 broadcast_in_dim.89
  229.2 3.6 %all-to-all-start.1 = ((f32[8,1,11520]{2,1,0:T(1,128)}), f32[8,1,11520]{2,1,0:T(1,128)S(1)}, u32[]{:S(2)}, u32[]{:S(2)}) async-start(f32[8,1,11520]{2,1,0:T(1,128)} %broadcast_in_dim.89), calls=%async_computation.1 | async-start | bytes 737280 | tf_op jit(solution)/shard_map/all_to_all | solution.py:29
  232.8 0.2 select_reduce_fusion
  233.0 11.4 %all-to-all-done.1 = f32[8,1,11520]{2,1,0:T(1,128)S(1)} async-done(((f32[8,1,11520]{2,1,0:T(1,128)}), f32[8,1,11520]{2,1,0:T(1,128)S(1)}, u32[]{:S(2)}, u32[]{:S(2)}) %all-to-all-start.1) | async-done | bytes 368672 | tf_op jit(solution)/shard_map/all_to_all | solution.py:29
  244.5 0.3 reduce_sum.169
  244.7 0.1 fusion.37
  244.8 0.6 fusion.64
  245.4 0.2 fusion.29
  245.6 0.8 copy.68
  246.5 9.4 %all-to-all-start.2 = ((f32[64,6,8]{2,1,0:T(8,128)}), f32[64,6,8]{2,1,0:T(8,128)S(1)}, u32[]{:S(2)}, u32[]{:S(2)}) async-start(f32[64,6,8]{2,1,0:T(8,128)} %copy.68), calls=%async_computation.2 | async-start | bytes 524288 | tf_op jit(solution)/shard_map/all_to_all | solution.py:52
  255.9 0.1 dynamic-slice_convert_fusion
  256.0 13.0 %all-to-all-done.2 = f32[64,6,8]{2,1,0:T(8,128)S(1)} async-done(((f32[64,6,8]{2,1,0:T(8,128)}), f32[64,6,8]{2,1,0:T(8,128)S(1)}, u32[]{:S(2)}, u32[]{:S(2)}) %all-to-all-start.2) | async-done | bytes 12320 | tf_op jit(solution)/shard_map/all_to_all | solution.py:52
  269.0 0.1 reduce_sum.174
  269.1 0.2 fusion.62
  269.3 0.2 multiply_reduce_fusion.1
  269.5 0.7 multiply_reduce_fusion.2
  270.2 3.2 %concatenate.7 = f32[5]{0:T(128)S(1)} concatenate(f32[1]{0:T(128)} %bitcast.21, f32[1]{0:T(128)} %bitcast.22, f32[1]{0:T(128)} %bitcast.23, f32[1]{0:T(128)} %bitcast.24, f32[1]{0:T(128)} %bitcast.25), dimensions={0} | concatenate | bytes 40 | tf_op jit(solution)/shard_map/concatenate | solution.py:41
  273.4 14.0 %all_to_all.22 = f32[64,1,5]{2,1,0:T(1,128)S(1)} all-to-all(f32[64,1,5]{2,1,0:T(1,128)S(1)} %broadcast_in_dim.93), channel_id=1, replica_groups=mesh['dp'=64,'mp'=8] {'dp'}, dimensions={0} | all-to-all | bytes 2560 | tf_op jit(solution)/shard_map/all_to_all | solution.py:29
  287.4 0.1 reduce_sum.182
  287.5 0.7 fusion.66
  292.1 0.5 subtract_multiply_fusion
  (22 shorter events, 0.2 us)
Async XLA Ops:
  0.6 62.3 %copy-start = (bf16[2048,256]{1,0:T(8,128)(2,1)S(1)}, bf16[2048,256]{1,0:T(8,128)(2,1)}, u32[]{:S(2)}) copy-start(bf16[2048,256]{1,0:T(8,128)(2,1)} %param.10) | copy-start | bytes 3145732
  0.6 62.3 %copy-start.1 = (bf16[15,128,256]{2,1,0:T(8,128)(2,1)S(1)}, bf16[15,128,256]{2,1,0:T(8,128)(2,1)}, u32[]{:S(2)}) copy-start(bf16[15,128,256]{2,1,0:T(8,128)(2,1)} %param.9) | copy-start | bytes 2949124
  0.7 33.3 %collective-permute-start.1 = (bf16[15,128,256]{2,1,0:T(8,128)(2,1)}, bf16[15,128,256]{2,1,0:T(8,128)(2,1)S(1)}, u32[]{:S(2)}, u32[]{:S(2)}) collective-permute-start(bf16[15,128,256]{2,1,0:T(8,128)(2,1)} %param.9), channel_id=1, source_target_pairs={{0,1},{1,2},{2,3},{3,4},{4,5},{5,6},{6,7},{7,0},{8,9},{9,10},{10,1... | collective-permute-start | bytes 2949128 | tf_op jit(solution)/shard_map/ppermute | solution.py:19
  5.6 30.3 %collective-permute-start = (bf16[15,128,256]{2,1,0:T(8,128)(2,1)}, bf16[15,128,256]{2,1,0:T(8,128)(2,1)}, u32[]{:S(2)}, u32[]{:S(2)}) collective-permute-start(bf16[15,128,256]{2,1,0:T(8,128)(2,1)} %param.9), channel_id=1, source_target_pairs={{0,7},{1,0},{2,1},{3,2},{4,3},{5,4},{6,5},{7,6},{8,15},{9,8},{10,9... | collective-permute-start | bytes 2949128 | tf_op jit(solution)/shard_map/ppermute | solution.py:21
  33.9 27.3 %copy-start.2 = (bf16[15,128,256]{2,1,0:T(8,128)(2,1)}, bf16[15,128,256]{2,1,0:T(8,128)(2,1)S(1)}, u32[]{:S(2)}) copy-start(bf16[15,128,256]{2,1,0:T(8,128)(2,1)S(1)} %collective-permute-done.1) | copy-start | bytes 2949124
  33.9 25.3 %collective-permute-start.3 = (bf16[15,128,256]{2,1,0:T(8,128)(2,1)S(1)}, bf16[15,128,256]{2,1,0:T(8,128)(2,1)}, u32[]{:S(2)}, u32[]{:S(2)}) collective-permute-start(bf16[15,128,256]{2,1,0:T(8,128)(2,1)S(1)} %collective-permute-done.1), channel_id=1, source_target_pairs={{0,1},{1,2},{2,3},{3,4},{4,5},{5,6},{6,7},{7,0},{8,9},{9,10},{10,1... | collective-permute-start | bytes 2949128 | tf_op jit(solution)/shard_map/ppermute | solution.py:19
  35.9 28.8 %collective-permute-start.2 = (bf16[15,128,256]{2,1,0:T(8,128)(2,1)}, bf16[15,128,256]{2,1,0:T(8,128)(2,1)}, u32[]{:S(2)}, u32[]{:S(2)}) collective-permute-start(bf16[15,128,256]{2,1,0:T(8,128)(2,1)} %collective-permute-done), channel_id=1, source_target_pairs={{0,7},{1,0},{2,1},{3,2},{4,3},{5,4},{6,5},{7,6},{8,15},{9,8},{10,9... | collective-permute-start | bytes 2949128 | tf_op jit(solution)/shard_map/ppermute | solution.py:21
  59.2 24.6 %collective-permute-start.5 = (bf16[15,128,256]{2,1,0:T(8,128)(2,1)}, bf16[15,128,256]{2,1,0:T(8,128)(2,1)}, u32[]{:S(2)}, u32[]{:S(2)}) collective-permute-start(bf16[15,128,256]{2,1,0:T(8,128)(2,1)} %collective-permute-done.3), channel_id=1, source_target_pairs={{0,1},{1,2},{2,3},{3,4},{4,5},{5,6},{6,7},{7,0},{8,9},{9,10},{10,1... | collective-permute-start | bytes 2949128 | tf_op jit(solution)/shard_map/ppermute | solution.py:19
  62.9 1.2 copy-start.3
  64.6 26.2 %collective-permute-start.4 = (bf16[15,128,256]{2,1,0:T(8,128)(2,1)}, bf16[15,128,256]{2,1,0:T(8,128)(2,1)S(1)}, u32[]{:S(2)}, u32[]{:S(2)}) collective-permute-start(bf16[15,128,256]{2,1,0:T(8,128)(2,1)} %collective-permute-done.2), channel_id=1, source_target_pairs={{0,7},{1,0},{2,1},{3,2},{4,3},{5,4},{6,5},{7,6},{8,15},{9,8},{10,9... | collective-permute-start | bytes 2949128 | tf_op jit(solution)/shard_map/ppermute | solution.py:21
  83.8 23.7 %collective-permute-start.6 = (bf16[15,128,256]{2,1,0:T(8,128)(2,1)}, bf16[15,128,256]{2,1,0:T(8,128)(2,1)S(1)}, u32[]{:S(2)}, u32[]{:S(2)}) collective-permute-start(bf16[15,128,256]{2,1,0:T(8,128)(2,1)} %collective-permute-done.5), channel_id=1, source_target_pairs={{0,1},{1,2},{2,3},{3,4},{4,5},{5,6},{6,7},{7,0},{8,9},{9,10},{10,1... | collective-permute-start | bytes 2949128 | tf_op jit(solution)/shard_map/ppermute | solution.py:19
  115.4 14.3 %copy-start.4 = (s32[960]{0:T(1024)S(1)}, s32[960]{0:T(1024)}, u32[]{:S(2)}) copy-start(s32[960]{0:T(1024)} %param.14) | copy-start | bytes 11524
  115.4 14.3 %copy-start.5 = (s32[960]{0:T(1024)S(1)}, s32[960]{0:T(1024)}, u32[]{:S(2)}) copy-start(s32[960]{0:T(1024)} %param.13) | copy-start | bytes 11524
  115.4 109.0 %all-to-all-start = ((bf16[64,128,256]{2,1,0:T(8,128)(2,1)}), bf16[64,128,256]{2,1,0:T(8,128)(2,1)}, u32[]{:S(2)}, u32[]{:S(2)}) async-start(bf16[64,128,256]{2,1,0:T(8,128)(2,1)} %copy.65), calls=%async_computation | async-start | bytes 8388608 | tf_op jit(solution)/shard_map/all_to_all | solution.py:110
  129.7 97.8 %copy-start.7 = (f32[256,8]{0,1:T(8,128)S(1)}, f32[256,8]{0,1:T(8,128)}, u32[]{:S(2)}) copy-start(f32[256,8]{0,1:T(8,128)} %param.12) | copy-start | bytes 24580
  129.7 97.8 %copy-start.8 = (f32[256]{0:T(256)S(1)}, f32[256]{0:T(256)}, u32[]{:S(2)}) copy-start(f32[256]{0:T(256)} %param.11) | copy-start | bytes 3076
  130.3 102.6 %copy-start.6 = (s32[384]{0:T(512)S(1)}, s32[384]{0:T(512)}, u32[]{:S(2)}) copy-start(s32[384]{0:T(512)} %param.15) | copy-start | bytes 4612
  229.2 15.3 %all-to-all-start.1 = ((f32[8,1,11520]{2,1,0:T(1,128)}), f32[8,1,11520]{2,1,0:T(1,128)S(1)}, u32[]{:S(2)}, u32[]{:S(2)}) async-start(f32[8,1,11520]{2,1,0:T(1,128)} %broadcast_in_dim.89), calls=%async_computation.1 | async-start | bytes 737280 | tf_op jit(solution)/shard_map/all_to_all | solution.py:29
  246.5 22.5 %all-to-all-start.2 = ((f32[64,6,8]{2,1,0:T(8,128)}), f32[64,6,8]{2,1,0:T(8,128)S(1)}, u32[]{:S(2)}, u32[]{:S(2)}) async-start(f32[64,6,8]{2,1,0:T(8,128)} %copy.68), calls=%async_computation.2 | async-start | bytes 524288 | tf_op jit(solution)/shard_map/all_to_all | solution.py:52
